TPU v7x, 32 devices: a whole 2x2x4 slice. The times are simulated.
32 devices in a mesh: wide: 8 (over y, x, core), narrow: 4 (over z).
Axes of the slice: x: 2, y: 2, z: 4, core: 2. Of those that a mesh axis runs over, the one named last changes fastest.
Arguments:
- layer_input: bfloat16 [4, 2048, 2048], P(None, 'wide'), may hold values from -6 to 6
- grad_out: bfloat16 [4, 2048, 2048], P(None, 'wide'), may hold values from -6 to 6
- lengths: int32 [4, 8], replicated, may hold values from 1 to 1024, 2048 in all within a row
- w_query: bfloat16 [2048, 2048], P('wide', 'narrow'), may hold values from -0.125 to 0.125
- w_key: bfloat16 [2048, 1024], P('wide', 'narrow'), may hold values from -0.125 to 0.125
- w_value: bfloat16 [2048, 1024], P('wide', 'narrow'), may hold values from -0.125 to 0.125
- w_out: bfloat16 [2048, 2048], P('narrow', 'wide'), may hold values from -0.75 to 0.75
- w_gate: bfloat16 [2048, 6144], P('wide', 'narrow'), may hold values from -0.125 to 0.125
- w_up: bfloat16 [2048, 6144], P('wide', 'narrow'), may hold values from -0.125 to 0.125
- w_down: bfloat16 [6144, 2048], P('narrow', 'wide'), may hold values from -0.078125 to 0.078125
- gain_attn: float32 [2048], replicated, may hold values from 0.25 to 1.75
- gain_ffn: float32 [2048], replicated, may hold values from 0.25 to 1.75
- gain_query: float32 [128], replicated, may hold values from 0.25 to 1.75
- gain_key: float32 [128], replicated, may hold values from 0.25 to 1.75
Outputs:
- output: bfloat16 [4, 2048, 2048], P(None, 'wide')
- grad_input: float32 [4, 2048, 2048], P(None, 'wide')
- grad_wquery: float32 [2048, 2048], P('wide', 'narrow')
- grad_wkey: float32 [2048, 1024], P('wide', 'narrow')
- grad_wvalue: float32 [2048, 1024], P('wide', 'narrow')
- grad_wout: float32 [2048, 2048], P('narrow', 'wide')
- grad_wgate: float32 [2048, 6144], P('wide', 'narrow')
- grad_wup: float32 [2048, 6144], P('wide', 'narrow')
- grad_wdown: float32 [6144, 2048], P('narrow', 'wide')
- grad_gattn: float32 [2048], replicated
- grad_gffn: float32 [2048], replicated
- grad_gquery: float32 [128], replicated
- grad_gkey: float32 [128], replicated
Inputs may be any that keep to these rules, and one draw needn't show every extreme that they name: `lengths`: each row cuts the 2048 tokens of its micro-batch into 8 consecutive pieces in order; pieces 0 to 6 are documents and the last piece is padding. A row's pieces sum to 2048, and its largest piece is exactly 1024.
All inputs are finite; a program needn't handle non-finite values.
Results may differ from a plain program's by a relative error of at most 0.022.
Values may be sent and summed in bfloat16 or wider, within the bound.
A program may use at most 256 MiB of HBM per device.

v0:
```python
import math
import jax
import jax.numpy as jnp
from jax import lax
from jax.sharding import PartitionSpec as P

HD = 128
NDOC = 8
EPSILON = 1e-06
THETA = 1000000.0


def rms_norm(values, gain):
    return values * lax.rsqrt(jnp.mean(values * values, axis=-1, keepdims=True) + EPSILON) * gain


def unit_rows(values):
    return values * lax.rsqrt(jnp.mean(values * values, axis=-1, keepdims=True) + EPSILON)


def rotate(values, cosine, sine):
    midway = values.shape[-1] // 2
    turned = jnp.concatenate([-values[..., midway:], values[..., :midway]], axis=-1)
    return values * cosine + turned * sine


def layout(lengths_row, total):
    finish = jnp.cumsum(lengths_row)
    starts = finish - lengths_row
    places = jnp.arange(total, dtype=jnp.int32)
    segment = jnp.sum((places[:, None] >= finish[None, :]).astype(jnp.int32), axis=1)
    member = segment[:, None] == jnp.arange(finish.shape[0], dtype=jnp.int32)[None, :]
    opening = jnp.sum(jnp.where(member, starts[None, :], 0), axis=1)
    return (segment, places - opening)


def angles(place):
    frequency = jnp.exp(-math.log(THETA) * jnp.arange(0, HD, 2).astype(jnp.float32) / HD)
    turning = place.astype(jnp.float32)[:, None] * frequency[None, :]
    turning = jnp.concatenate([turning, turning], axis=-1)
    return (jnp.cos(turning), jnp.sin(turning))


def allowed(query_seg, query_idx, key_seg, key_idx):
    same_doc = query_seg[:, None] == key_seg[None, :]
    causal = key_idx[None, :] <= query_idx[:, None]
    usable = (key_seg[None, :] != NDOC - 1) | (key_idx[None, :] == query_idx[:, None])
    return same_doc & causal & usable


def attention_scores(query_low, key_all, mask_local, factor):
    scores = (
        jnp.einsum("tgrd,kgd->grtk", query_low, key_all, preferred_element_type=jnp.float32)
        * factor
    )
    return jnp.where(mask_local[None, None], scores, -1e30)


def one_batch(row_input, grad_row, lengths_row, gathered, gains):
    w_query, w_key, w_value, w_out, w_gate, w_up, w_down = gathered
    gain_attn, gain_ffn, gain_query, gain_key = gains
    tok_rows = row_input.shape[0]
    total = tok_rows * lax.axis_size("wide")
    groups = w_key.shape[1] // HD
    repeat = w_query.shape[1] // w_key.shape[1]
    factor = 1.0 / math.sqrt(HD)
    first_row = lax.axis_index("wide") * tok_rows
    segment, place = layout(lengths_row, total)
    positions = jnp.arange(total, dtype=jnp.int32)
    query_seg = lax.dynamic_slice_in_dim(segment, first_row, tok_rows)
    query_idx = lax.dynamic_slice_in_dim(positions, first_row, tok_rows)
    mask_local = allowed(query_seg, query_idx, segment, positions)
    cosine, sine = angles(lax.dynamic_slice_in_dim(place, first_row, tok_rows))

    def head_norm(rows, gain):
        return rotate(rms_norm(rows, gain), cosine[:, None, :], sine[:, None, :])

    input_float = row_input.astype(jnp.float32)
    grad_float = grad_row.astype(jnp.float32)
    normed_one, pull_one = jax.vjp(lambda rows: rms_norm(rows, gain_attn), input_float)
    hidden_one = normed_one.astype(jnp.bfloat16)
    query_raw = jnp.dot(hidden_one, w_query, preferred_element_type=jnp.float32).reshape(
        tok_rows, groups * repeat, HD
    )
    key_raw = jnp.dot(hidden_one, w_key, preferred_element_type=jnp.float32).reshape(
        tok_rows, groups, HD
    )
    value_low = jnp.dot(hidden_one, w_value, preferred_element_type=jnp.float32).astype(
        jnp.bfloat16
    )
    query_turned, pull_query = jax.vjp(head_norm, query_raw, gain_query)
    key_turned, pull_key = jax.vjp(head_norm, key_raw, gain_key)
    query_low = query_turned.astype(jnp.bfloat16).reshape(tok_rows, groups, repeat, HD)
    key_low = key_turned.astype(jnp.bfloat16).reshape(tok_rows, groups * HD)
    key_all, value_all = (
        lax.all_gather(key_low, "wide", axis=0, tiled=True),
        lax.all_gather(value_low, "wide", axis=0, tiled=True),
    )
    key_all = key_all.reshape(total, groups, HD)
    value_all = value_all.reshape(total, groups, HD)
    scores = attention_scores(query_low, key_all, mask_local, factor)
    highest = jnp.max(scores, axis=-1, keepdims=True)
    exponent = jnp.exp(scores - highest)
    denominator = jnp.sum(exponent, axis=-1, keepdims=True)
    log_total = highest + jnp.log(denominator)
    probs_low = (exponent / denominator).astype(jnp.bfloat16)
    mixed = jnp.einsum("grtk,kgd->tgrd", probs_low, value_all, preferred_element_type=jnp.float32)
    mixed_low = mixed.reshape(tok_rows, groups * repeat * HD).astype(jnp.bfloat16)
    attn_part = jnp.dot(mixed_low, w_out, preferred_element_type=jnp.float32)
    middle = input_float + lax.psum(attn_part.astype(jnp.bfloat16), "narrow").astype(jnp.float32)
    normed_two, pull_two = jax.vjp(lambda rows: rms_norm(rows, gain_ffn), middle)
    hidden_two = normed_two.astype(jnp.bfloat16)
    unit_two = unit_rows(middle)
    gate = jnp.dot(hidden_two, w_gate, preferred_element_type=jnp.float32)
    up_proj = jnp.dot(hidden_two, w_up, preferred_element_type=jnp.float32)
    active, pull_active = jax.vjp(
        lambda gate_in, up_in: jax.nn.silu(gate_in) * up_in, gate, up_proj
    )
    active_low = active.astype(jnp.bfloat16)
    ffn_part = jnp.dot(active_low, w_down, preferred_element_type=jnp.float32)
    output_low = (
        middle + lax.psum(ffn_part.astype(jnp.bfloat16), "narrow").astype(jnp.float32)
    ).astype(jnp.bfloat16)
    grad_wdown = jnp.einsum("tf,td->fd", active_low, grad_row, preferred_element_type=jnp.float32)
    grad_active = jnp.einsum("td,fd->tf", grad_row, w_down, preferred_element_type=jnp.float32)
    grad_gate, grad_upper = pull_active(grad_active)
    gate_back = grad_gate.astype(jnp.bfloat16)
    upper_back = grad_upper.astype(jnp.bfloat16)
    grad_wgate = jnp.einsum("td,tf->df", hidden_two, gate_back, preferred_element_type=jnp.float32)
    grad_wup = jnp.einsum("td,tf->df", hidden_two, upper_back, preferred_element_type=jnp.float32)
    partial_two = jnp.einsum(
        "tf,df->td", gate_back, w_gate, preferred_element_type=jnp.float32
    ) + jnp.einsum("tf,df->td", upper_back, w_up, preferred_element_type=jnp.float32)
    gain_two = jnp.sum(partial_two * unit_two, axis=0)
    grad_middle = (
        grad_float
        + pull_two(lax.psum(partial_two.astype(jnp.bfloat16), "narrow").astype(jnp.float32))[0]
    )
    middle_low = grad_middle.astype(jnp.bfloat16)
    grad_wout = jnp.einsum("th,td->hd", mixed_low, middle_low, preferred_element_type=jnp.float32)
    grad_mixed = jnp.einsum("td,hd->th", middle_low, w_out, preferred_element_type=jnp.float32)
    grad_mixed = grad_mixed.astype(jnp.bfloat16).reshape(tok_rows, groups, repeat, HD)
    scores = attention_scores(query_low, key_all, mask_local, factor)
    probs = jnp.exp(scores - log_total)
    grad_probs = jnp.einsum(
        "tgrd,kgd->grtk", grad_mixed, value_all, preferred_element_type=jnp.float32
    )
    weighted = jnp.sum(probs * grad_probs, axis=-1, keepdims=True)
    grad_scores = (probs * (grad_probs - weighted)).astype(jnp.bfloat16)
    grad_turned = (
        jnp.einsum("grtk,kgd->tgrd", grad_scores, key_all, preferred_element_type=jnp.float32)
        * factor
    )
    grad_keyall = (
        jnp.einsum("grtk,tgrd->kgd", grad_scores, query_low, preferred_element_type=jnp.float32)
        * factor
    )
    grad_valueall = jnp.einsum(
        "grtk,tgrd->kgd", probs.astype(jnp.bfloat16), grad_mixed, preferred_element_type=jnp.float32
    )
    grad_keys, grad_values = (
        lax.psum_scatter(
            grad_keyall.reshape(total, groups * HD).astype(jnp.bfloat16),
            "wide",
            scatter_dimension=0,
            tiled=True,
        ).astype(jnp.float32),
        lax.psum_scatter(
            grad_valueall.reshape(total, groups * HD).astype(jnp.bfloat16),
            "wide",
            scatter_dimension=0,
            tiled=True,
        ).astype(jnp.float32),
    )
    grad_qraw, gain_q = pull_query(grad_turned.reshape(tok_rows, groups * repeat, HD))
    grad_kraw, gain_k = pull_key(grad_keys.reshape(tok_rows, groups, HD))
    query_back = grad_qraw.reshape(tok_rows, groups * repeat * HD).astype(jnp.bfloat16)
    key_back = grad_kraw.reshape(tok_rows, groups * HD).astype(jnp.bfloat16)
    value_back = grad_values.astype(jnp.bfloat16)
    grad_wquery = jnp.einsum(
        "td,th->dh", hidden_one, query_back, preferred_element_type=jnp.float32
    )
    grad_wkey = jnp.einsum("td,th->dh", hidden_one, key_back, preferred_element_type=jnp.float32)
    grad_wvalue = jnp.einsum(
        "td,th->dh", hidden_one, value_back, preferred_element_type=jnp.float32
    )
    partial_one = (
        jnp.einsum("th,dh->td", query_back, w_query, preferred_element_type=jnp.float32)
        + jnp.einsum("th,dh->td", key_back, w_key, preferred_element_type=jnp.float32)
        + jnp.einsum("th,dh->td", value_back, w_value, preferred_element_type=jnp.float32)
    )
    gain_one = jnp.sum(partial_one * unit_rows(input_float), axis=0)
    grad_input = (
        grad_middle
        + pull_one(lax.psum(partial_one.astype(jnp.bfloat16), "narrow").astype(jnp.float32))[0]
    )
    weight_grads = (
        grad_wquery,
        grad_wkey,
        grad_wvalue,
        grad_wout,
        grad_wgate,
        grad_wup,
        grad_wdown,
    )
    return (output_low, grad_input, weight_grads, (gain_one, gain_two, gain_q, gain_k))


def local(
    layer_input,
    grad_out,
    lengths,
    w_query,
    w_key,
    w_value,
    w_out,
    w_gate,
    w_up,
    w_down,
    gain_attn,
    gain_ffn,
    gain_query,
    gain_key,
):
    width = lax.axis_size("wide")
    shards = (w_query, w_key, w_value, w_out, w_gate, w_up, w_down)
    along_rows = (True, True, True, False, True, True, False)
    gains = (gain_attn, gain_ffn, gain_query, gain_key)
    totals = tuple(
        (
            jnp.zeros(
                (
                    (piece.shape[0] * width, piece.shape[1])
                    if rows_first
                    else (piece.shape[0], piece.shape[1] * width)
                ),
                jnp.float32,
            )
            for piece, rows_first in zip(shards, along_rows)
        )
    )
    gain_terms = tuple((jnp.zeros(gain.shape, jnp.float32) for gain in gains))
    outputs = []
    grad_inputs = []
    for micro in range(layer_input.shape[0]):
        gathered = (
            lax.all_gather(w_query, "wide", axis=0, tiled=True),
            lax.all_gather(w_key, "wide", axis=0, tiled=True),
            lax.all_gather(w_value, "wide", axis=0, tiled=True),
            lax.all_gather(w_out, "wide", axis=1, tiled=True),
            lax.all_gather(w_gate, "wide", axis=0, tiled=True),
            lax.all_gather(w_up, "wide", axis=0, tiled=True),
            lax.all_gather(w_down, "wide", axis=1, tiled=True),
        )
        output, grad_input, weight_grads, gain_grads = one_batch(
            layer_input[micro], grad_out[micro], lengths[micro], gathered, gains
        )
        outputs.append(output)
        grad_inputs.append(grad_input)
        gain_terms = tuple((running + fresh for running, fresh in zip(gain_terms, gain_grads)))
        totals = tuple((running + fresh for running, fresh in zip(totals, weight_grads)))
    results = (
        lax.psum_scatter(
            totals[0].astype(jnp.bfloat16), "wide", scatter_dimension=0, tiled=True
        ).astype(jnp.float32),
        lax.psum_scatter(
            totals[1].astype(jnp.bfloat16), "wide", scatter_dimension=0, tiled=True
        ).astype(jnp.float32),
        lax.psum_scatter(
            totals[2].astype(jnp.bfloat16), "wide", scatter_dimension=0, tiled=True
        ).astype(jnp.float32),
        lax.psum_scatter(
            totals[3].astype(jnp.bfloat16), "wide", scatter_dimension=1, tiled=True
        ).astype(jnp.float32),
        lax.psum_scatter(
            totals[4].astype(jnp.bfloat16), "wide", scatter_dimension=0, tiled=True
        ).astype(jnp.float32),
        lax.psum_scatter(
            totals[5].astype(jnp.bfloat16), "wide", scatter_dimension=0, tiled=True
        ).astype(jnp.float32),
        lax.psum_scatter(
            totals[6].astype(jnp.bfloat16), "wide", scatter_dimension=1, tiled=True
        ).astype(jnp.float32),
    )
    gain_total = lax.psum(gain_terms, ("wide", "narrow"))
    return (
        jnp.stack(outputs),
        jnp.stack(grad_inputs),
        results[0],
        results[1],
        results[2],
        results[3],
        results[4],
        results[5],
        results[6],
        gain_total[0],
        gain_total[1],
        gain_total[2],
        gain_total[3],
    )


def solution(mesh):
    in_specs = (
        P(None, "wide", None),
        P(None, "wide", None),
        P(),
        P("wide", "narrow"),
        P("wide", "narrow"),
        P("wide", "narrow"),
        P("narrow", "wide"),
        P("wide", "narrow"),
        P("wide", "narrow"),
        P("narrow", "wide"),
        P(),
        P(),
        P(),
        P(),
    )
    out_specs = (
        P(None, "wide", None),
        P(None, "wide", None),
        P("wide", "narrow"),
        P("wide", "narrow"),
        P("wide", "narrow"),
        P("narrow", "wide"),
        P("wide", "narrow"),
        P("wide", "narrow"),
        P("narrow", "wide"),
        P(),
        P(),
        P(),
        P(),
    )
    return jax.shard_map(local, mesh=mesh, in_specs=in_specs, out_specs=out_specs, check_vma=False)
```

profile of v0, /device:TPU:0, one launch (start us, length us, event | category | flops | bytes accessed | tf_op | source)
XLA Modules:
  0.0 1960.0 jit_solution(11782084816646856816)
XLA Ops:
  14.2 21.9 %all-gather.16.cloned.1.call-done = bf16[2048,256]{1,0:T(8,128)(2,1)} async-done(((bf16[256,256]{1,0:T(8,128)(2,1)}), bf16[2048,256]{1,0:T(8,128)(2,1)}) %all-gather.16.cloned.1.call-update) | async-done | bytes 1048592 | tf_op jit(solution)/shard_map/all_gather | solution.py:249
  39.5 21.8 %all-gather.20.cloned.1.call-done = bf16[2048,256]{1,0:T(8,128)(2,1)} async-done(((bf16[256,256]{1,0:T(8,128)(2,1)}), bf16[2048,256]{1,0:T(8,128)(2,1)}) %all-gather.20.cloned.1.call-update) | async-done | bytes 1048592 | tf_op jit(solution)/shard_map/all_gather | solution.py:248
  94.9 21.8 %all-gather.38.cloned.1.call-done = bf16[2048,256]{1,0:T(8,128)(2,1)} async-done(((bf16[256,256]{1,0:T(8,128)(2,1)}), bf16[2048,256]{1,0:T(8,128)(2,1)}) %all-gather.38.cloned.1.call-update) | async-done | bytes 1048592 | tf_op jit(solution)/shard_map/all_gather | solution.py:97
  122.2 20.3 %all-gather.40.cloned.1.call-done = bf16[2048,256]{0,1:T(8,128)(2,1)} async-done(((bf16[256,256]{0,1:T(8,128)(2,1)}), bf16[2048,256]{0,1:T(8,128)(2,1)}) %all-gather.40.cloned.1.call-update) | async-done | bytes 1048592 | tf_op jit(solution)/shard_map/all_gather | solution.py:96
  150.4 22.0 %all-gather.26.cloned.1.call-done = bf16[512,2048]{1,0:T(8,128)(2,1)} async-done(((bf16[512,256]{1,0:T(8,128)(2,1)}), bf16[512,2048]{1,0:T(8,128)(2,1)}) %all-gather.26.cloned.1.call-update) | async-done | bytes 2097168 | tf_op jit(solution)/shard_map/all_gather | solution.py:250
  175.8 52.0 %all-reduce.25.cloned.1.call-done = bf16[256,2048]{1,0:T(8,128)(2,1)} async-done(((bf16[256,2048]{1,0:T(8,128)(2,1)}), bf16[256,2048]{1,0:T(8,128)(2,1)}) %all-reduce.25.cloned.1.call-update) | async-done | bytes 1048592 | tf_op jit(solution)/shard_map/psum | solution.py:110
  262.1 20.4 %all-gather.18.cloned.1.call-done = bf16[2048,256]{1,0:T(8,128)(2,1)} async-done(((bf16[256,256]{1,0:T(8,128)(2,1)}), bf16[2048,256]{1,0:T(8,128)(2,1)}) %all-gather.18.cloned.1.call-update) | async-done | bytes 1048592 | tf_op jit(solution)/shard_map/all_gather | solution.py:97
  284.6 23.5 %all-gather.34.cloned.1.call-done = bf16[2048,256]{1,0:T(8,128)(2,1)} async-done(((bf16[256,256]{1,0:T(8,128)(2,1)}), bf16[2048,256]{1,0:T(8,128)(2,1)}) %all-gather.34.cloned.1.call-update) | async-done | bytes 1048592 | tf_op jit(solution)/shard_map/all_gather | solution.py:97
  310.5 23.6 %all-gather.44.cloned.1.call-done = bf16[2048,256]{0,1:T(8,128)(2,1)} async-done(((bf16[256,256]{0,1:T(8,128)(2,1)}), bf16[2048,256]{0,1:T(8,128)(2,1)}) %all-gather.44.cloned.1.call-update) | async-done | bytes 1048592 | tf_op jit(solution)/shard_map/all_gather | solution.py:96
  395.0 36.9 %all-gather.28.cloned.1.call-done = bf16[2048,1536]{1,0:T(8,128)(2,1)} async-done(((bf16[256,1536]{1,0:T(8,128)(2,1)}), bf16[2048,1536]{1,0:T(8,128)(2,1)}) %all-gather.28.cloned.1.call-update) | async-done | bytes 6291472 | tf_op jit(solution)/shard_map/all_gather | solution.py:251
  437.6 42.6 %all-gather.32.cloned.1.call-done = bf16[1536,2048]{1,0:T(8,128)(2,1)} async-done(((bf16[1536,256]{1,0:T(8,128)(2,1)}), bf16[1536,2048]{1,0:T(8,128)(2,1)}) %all-gather.32.cloned.1.call-update) | async-done | bytes 6291472 | tf_op jit(solution)/shard_map/all_gather | solution.py:253
  486.3 41.1 %all-gather.30.cloned.1.call-done = bf16[2048,1536]{1,0:T(8,128)(2,1)} async-done(((bf16[256,1536]{1,0:T(8,128)(2,1)}), bf16[2048,1536]{1,0:T(8,128)(2,1)}) %all-gather.30.cloned.1.call-update) | async-done | bytes 6291472 | tf_op jit(solution)/shard_map/all_gather | solution.py:252
  543.0 155.1 %all-reduce.31.cloned.1.call-done = (bf16[256,2048]{1,0:T(8,128)(2,1)}, bf16[256,2048]{1,0:T(8,128)(2,1)}, bf16[256,2048]{1,0:T(8,128)(2,1)}, bf16[256,2048]{1,0:T(8,128)(2,1)}) async-done(((bf16[256,2048]{1,0:T(8,128)(2,1)}, bf16[256,2048]{1,0:T(8,128)(2,1)}, bf16[256,2048]{1,0:T(8,128)(2,1)}, bf16[256,2048]{1,0:T(8,128)(2,1)}), (bf16[256,2048]{1,0:T(8,128)(2,1)}, bf16[256,2048]{1,0:T(8,128)(2,1)}, ...) | async-done | bytes 4194320 | tf_op jit(solution)/shard_map/psum | solution.py:110
  770.9 119.5 %all-reduce.29.cloned.1.call-done = (bf16[256,2048]{1,0:T(8,128)(2,1)}, bf16[256,2048]{1,0:T(8,128)(2,1)}, bf16[256,2048]{1,0:T(8,128)(2,1)}) async-done(((bf16[256,2048]{1,0:T(8,128)(2,1)}, bf16[256,2048]{1,0:T(8,128)(2,1)}, bf16[256,2048]{1,0:T(8,128)(2,1)}), (bf16[256,2048]{1,0:T(8,128)(2,1)}, bf16[256,2048]{1,0:T(8,128)(2,1)}, bf16[256,2048]{1,0:T(8,128)(2,1)})) %all-reduce.29.cloned.1.call-update) | async-done | bytes 3145744 | tf_op jit(solution)/shard_map/psum | solution.py:137
  1091.6 22.0 %reduce-scatter.18.cloned.1.call-done = bf16[256,256]{0,1:T(8,128)(2,1)} async-done(((bf16[2048,256]{0,1:T(8,128)(2,1)}), bf16[256,256]{0,1:T(8,128)(2,1)}) %reduce-scatter.18.cloned.1.call-update) | async-done | bytes 131088 | tf_op jit(solution)/shard_map/reduce_scatter | solution.py:168
  1116.7 35.9 %reduce-scatter.22.cloned.1.call-done = bf16[256,256]{0,1:T(8,128)(2,1)} async-done(((bf16[2048,256]{0,1:T(8,128)(2,1)}), bf16[256,256]{0,1:T(8,128)(2,1)}) %reduce-scatter.22.cloned.1.call-update) | async-done | bytes 131088 | tf_op jit(solution)/shard_map/reduce_scatter | solution.py:168
  1156.5 35.3 %reduce-scatter.26.cloned.1.call-done = bf16[256,256]{0,1:T(8,128)(2,1)} async-done(((bf16[2048,256]{0,1:T(8,128)(2,1)}), bf16[256,256]{0,1:T(8,128)(2,1)}) %reduce-scatter.26.cloned.1.call-update) | async-done | bytes 131088 | tf_op jit(solution)/shard_map/reduce_scatter | solution.py:168
  1195.7 35.7 %reduce-scatter.30.cloned.1.call-done = bf16[256,256]{0,1:T(8,128)(2,1)} async-done(((bf16[2048,256]{0,1:T(8,128)(2,1)}), bf16[256,256]{0,1:T(8,128)(2,1)}) %reduce-scatter.30.cloned.1.call-update) | async-done | bytes 131088 | tf_op jit(solution)/shard_map/reduce_scatter | solution.py:168
  1372.4 27.0 %reduce-scatter.36.cloned.1.call-done = bf16[256,256]{1,0:T(8,128)(2,1)} async-done(((bf16[2048,256]{1,0:T(8,128)(2,1)}), bf16[256,256]{1,0:T(8,128)(2,1)}) %reduce-scatter.36.cloned.1.call-update) | async-done | bytes 131088 | tf_op jit(solution)/shard_map/reduce_scatter | solution.py:269
  1401.1 64.1 %reduce-scatter.40.cloned.1.call-done = bf16[256,1536]{1,0:T(8,128)(2,1)} async-done(((bf16[2048,1536]{1,0:T(8,128)(2,1)}), bf16[256,1536]{1,0:T(8,128)(2,1)}) %reduce-scatter.40.cloned.1.call-update) | async-done | bytes 786448 | tf_op jit(solution)/shard_map/reduce_scatter | solution.py:275
  1467.7 62.7 %reduce-scatter.42.cloned.1.call-done = bf16[256,1536]{1,0:T(8,128)(2,1)} async-done(((bf16[2048,1536]{1,0:T(8,128)(2,1)}), bf16[256,1536]{1,0:T(8,128)(2,1)}) %reduce-scatter.42.cloned.1.call-update) | async-done | bytes 786448 | tf_op jit(solution)/shard_map/reduce_scatter | solution.py:278
  1532.9 62.4 %reduce-scatter.44.cloned.1.call-done = bf16[1536,256]{1,0:T(8,128)(2,1)} async-done(((bf16[1536,2048]{1,0:T(8,128)(2,1)}), bf16[1536,256]{1,0:T(8,128)(2,1)}) %reduce-scatter.44.cloned.1.call-update) | async-done | bytes 786448 | tf_op jit(solution)/shard_map/reduce_scatter | solution.py:281
  1597.7 292.1 %all-reduce.27.cloned.1.call-done = (bf16[256,2048]{1,0:T(8,128)(2,1)}, bf16[256,2048]{1,0:T(8,128)(2,1)}, bf16[256,2048]{1,0:T(8,128)(2,1)}, bf16[256,2048]{1,0...) async-done(((bf16[256,2048]{1,0:T(8,128)(2,1)}, bf16[256,2048]{1,0:T(8,128)(2,1)}, ...) | async-done | bytes 8388624 | tf_op jit(solution)/shard_map/psum | solution.py:122
  1913.2 39.5 %all-reduce.16 = (f32[2048]{0:T(1024)}, f32[2048]{0:T(1024)}, f32[128]{0:T(128)}, f32[128]{0:T(128)}) all-reduce(f32[2048]{0:T(1024)S(1)} %add_add_fusion.17, f32[2048]{0:T(1024)S(1)} %add_add_fusion.16, f32[128]{0:T(128)S(1)} %add_add_fusion.19, f32[128]{0:T(128)S(1)} %add_add_fusion.18), channel_id=1, replica_groups=mesh['wide'=8,'narrow'=4] {'wide','narrow'}, use_global_device_ids=true, to_apply=%region_91.92 | all-reduce | flops 4352 | bytes 34816 | tf_op jit(solution)/shard_map/psum | solution.py:285
  (874 shorter events, 642.5 us)
Async XLA Ops:
  67.1 160.7 %all-reduce.25.cloned.1.call-start = ((), (), s32[]{:S(2)}) async-start(), calls=%async_computation.28 | async-start | bytes 2097152 | tf_op jit(solution)/shard_map/psum | solution.py:110
  246.5 112.8 %all-gather.22.cloned.1.call-start = ((), (), s32[]{:S(2)}) async-start(), calls=%async_computation.18 | async-start | bytes 1179648 | tf_op jit(solution)/shard_map/all_gather | solution.py:96
  247.9 136.9 %all-gather.36.cloned.1.call-start = ((), (), s32[]{:S(2)}) async-start(), calls=%async_computation.25 | async-start | bytes 1179648 | tf_op jit(solution)/shard_map/all_gather | solution.py:96
  249.2 182.8 %all-gather.28.cloned.1.call-start = ((), (), s32[]{:S(2)}) async-start(), calls=%async_computation.21 | async-start | bytes 7077888 | tf_op jit(solution)/shard_map/all_gather | solution.py:251
  249.7 230.5 %all-gather.32.cloned.1.call-start = ((), (), s32[]{:S(2)}) async-start(), calls=%async_computation.23 | async-start | bytes 7077888 | tf_op jit(solution)/shard_map/all_gather | solution.py:253
  250.3 277.1 %all-gather.30.cloned.1.call-start = ((), (), s32[]{:S(2)}) async-start(), calls=%async_computation.22 | async-start | bytes 7077888 | tf_op jit(solution)/shard_map/all_gather | solution.py:252
  250.9 447.3 %all-reduce.31.cloned.1.call-start = ((), (), s32[]{:S(2)}) async-start(), calls=%async_computation.48 | async-start | bytes 8388608 | tf_op jit(solution)/shard_map/psum | solution.py:110
  543.0 347.4 %all-reduce.29.cloned.1.call-start = ((), (), s32[]{:S(2)}) async-start(), calls=%async_computation.47 | async-start | bytes 6291456 | tf_op jit(solution)/shard_map/psum | solution.py:137
  770.1 278.1 %reduce-scatter.24.cloned.1.call-start = ((), (), s32[]{:S(2)}) async-start(), calls=%async_computation.35 | async-start | bytes 1179648 | tf_op jit(solution)/shard_map/reduce_scatter | solution.py:162
  920.7 129.1 %reduce-scatter.16.cloned.1.call-start = ((), (), s32[]{:S(2)}) async-start(), calls=%async_computation.31 | async-start | bytes 1179648 | tf_op jit(solution)/shard_map/reduce_scatter | solution.py:162
  941.9 109.7 %reduce-scatter.28.cloned.1.call-start = ((), (), s32[]{:S(2)}) async-start(), calls=%async_computation.37 | async-start | bytes 1179648 | tf_op jit(solution)/shard_map/reduce_scatter | solution.py:162
  958.9 114.9 %reduce-scatter.20.cloned.1.call-start = ((), (), s32[]{:S(2)}) async-start(), calls=%async_computation.33 | async-start | bytes 1179648 | tf_op jit(solution)/shard_map/reduce_scatter | solution.py:162
  969.1 144.5 %reduce-scatter.18.cloned.1.call-start = ((), (), s32[]{:S(2)}) async-start(), calls=%async_computation.32 | async-start | bytes 1179648 | tf_op jit(solution)/shard_map/reduce_scatter | solution.py:168
  980.4 172.2 %reduce-scatter.22.cloned.1.call-start = ((), (), s32[]{:S(2)}) async-start(), calls=%async_computation.34 | async-start | bytes 1179648 | tf_op jit(solution)/shard_map/reduce_scatter | solution.py:168
  991.2 200.6 %reduce-scatter.26.cloned.1.call-start = ((), (), s32[]{:S(2)}) async-start(), calls=%async_computation.36 | async-start | bytes 1179648 | tf_op jit(solution)/shard_map/reduce_scatter | solution.py:168
  1003.1 228.3 %reduce-scatter.30.cloned.1.call-start = ((), (), s32[]{:S(2)}) async-start(), calls=%async_computation.38 | async-start | bytes 1179648 | tf_op jit(solution)/shard_map/reduce_scatter | solution.py:168
  1017.1 349.9 %reduce-scatter.32.cloned.1.call-start = ((), (), s32[]{:S(2)}) async-start(), calls=%async_computation.39 | async-start | bytes 2359296 | tf_op jit(solution)/shard_map/reduce_scatter | solution.py:263
  1025.6 343.1 %reduce-scatter.38.cloned.1.call-start = ((), (), s32[]{:S(2)}) async-start(), calls=%async_computation.42 | async-start | bytes 2359296 | tf_op jit(solution)/shard_map/reduce_scatter | solution.py:272
  1048.1 322.7 %reduce-scatter.34.cloned.1.call-start = ((), (), s32[]{:S(2)}) async-start(), calls=%async_computation.40 | async-start | bytes 1179648 | tf_op jit(solution)/shard_map/reduce_scatter | solution.py:266
  1083.6 315.9 %reduce-scatter.36.cloned.1.call-start = ((), (), s32[]{:S(2)}) async-start(), calls=%async_computation.41 | async-start | bytes 1179648 | tf_op jit(solution)/shard_map/reduce_scatter | solution.py:269
  1235.0 230.2 %reduce-scatter.40.cloned.1.call-start = ((), (), s32[]{:S(2)}) async-start(), calls=%async_computation.43 | async-start | bytes 7077888 | tf_op jit(solution)/shard_map/reduce_scatter | solution.py:275
  1253.3 277.1 %reduce-scatter.42.cloned.1.call-start = ((), (), s32[]{:S(2)}) async-start(), calls=%async_computation.44 | async-start | bytes 7077888 | tf_op jit(solution)/shard_map/reduce_scatter | solution.py:278
  1291.8 303.5 %reduce-scatter.44.cloned.1.call-start = ((), (), s32[]{:S(2)}) async-start(), calls=%async_computation.45 | async-start | bytes 7077888 | tf_op jit(solution)/shard_map/reduce_scatter | solution.py:281
  1330.8 559.0 %all-reduce.27.cloned.1.call-start = ((), (), s32[]{:S(2)}) async-start(), calls=%async_computation.46 | async-start | bytes 16777216 | tf_op jit(solution)/shard_map/psum | solution.py:122
  (275 other events, 3599.1 us)
Sparse Core Ops, SparseCore 0:
  63.2 27.7 all-gather.23
  144.3 28.0 all-gather.25
  175.8 51.8 all-reduce.24
  386.5 45.3 all-gather.27
  433.6 46.5 all-gather.31
  482.0 45.3 all-gather.29
  543.1 155.0 all-reduce.30
  770.3 120.0 all-reduce.28
  920.9 34.9 reduce-scatter.23
  959.5 35.9 reduce-scatter.15
  998.7 35.9 reduce-scatter.27
  1037.8 35.9 reduce-scatter.19
  1077.6 35.9 reduce-scatter.17
  1116.6 35.9 reduce-scatter.21
  1155.8 35.9 reduce-scatter.25
  1195.4 35.9 reduce-scatter.29
  1234.5 41.1 reduce-scatter.31
  1279.0 41.1 reduce-scatter.37
  1323.9 35.9 reduce-scatter.33
  1363.5 35.9 reduce-scatter.35
  1403.4 61.7 reduce-scatter.39
  1468.6 61.7 reduce-scatter.41
  1533.7 61.5 reduce-scatter.43
  1598.7 291.0 all-reduce.26
  (10 shorter events, 235.5 us)
where the time goes:
time: 1970 us; the launch traced here: 1960 us
  waiting for transfers between devices  1330 us (68%)
  matrix products  388 us (20%)
  other arithmetic  128 us (6%)
  local copies, waits for them, and re-layouts  54.3 us (3%)
  blocking collectives  39.5 us (2%)
    psum x1, waiting for transfers between devices, one_batch(): lax.psum(ffn_part.astype(jnp.bfloat16), 'narrow').astype(jnp.float32)  292 us
    psum x2, waiting for transfers between devices, one_batch(): lax.psum(attn_part.astype(jnp.bfloat16), 'narrow').astype(jnp.float32)  207 us
    reduce_scatter x4, waiting for transfers between devices, one_batch(): lax.psum_scatter(grad_valueall.reshape(total, groups * HD).astype(jnp.bfl...  129 us
    psum x1, waiting for transfers between devices, one_batch(): lax.psum(partial_two.astype(jnp.bfloat16), 'narrow').astype(jnp.float32)  119 us
    all_gather x4, waiting for transfers between devices, one_batch(): lax.all_gather(key_low, 'wide', axis=0, tiled=True)  74 us
    all_gather x4, waiting for transfers between devices, one_batch(): lax.all_gather(value_low, 'wide', axis=0, tiled=True)  65.8 us
    reduce_scatter x1, waiting for transfers between devices, local(): lax.psum_scatter(totals[4].astype(jnp.bfloat16), 'wide', scatter_dimensio...  64.1 us
    reduce_scatter x1, waiting for transfers between devices, local(): lax.psum_scatter(totals[5].astype(jnp.bfloat16), 'wide', scatter_dimensio...  62.7 us
  transfers between devices with their start and end apart: 34, of which 28 were waited for; matrix products, arithmetic and copies ran while one was open for 20% of the time, Pallas kernels for 0%

commit v1 on v0

--- a/solution.py
+++ b/solution.py
@@ -8,6 +8,28 @@
 NDOC = 8
 EPSILON = 1e-06
 THETA = 1000000.0
+
+
+def laid_out(blocks, dim):
+    shape = list(blocks.shape[1:])
+    shape[dim] *= blocks.shape[0]
+    return jnp.moveaxis(blocks, 0, dim).reshape(shape)
+
+
+def collect(x, axis, dim):
+    size = lax.axis_size(axis)
+    pairs = [(i, (i + 1) % size) for i in range(size)]
+    back = [(b, a) for a, b in pairs]
+    lower, upper = ([], [])
+    for hop in range(size - 1):
+        if hop % 2 == 0:
+            lower.append(lax.ppermute(lower[-1] if lower else x, axis, pairs))
+        else:
+            upper.append(lax.ppermute(upper[-1] if upper else x, axis, back))
+    tiles = jnp.stack([*lower[::-1], x, *upper])
+    shift = lax.axis_index(axis) - len(lower)
+    tiles = tiles[(jnp.arange(size) - shift) % size]
+    return laid_out(tiles, dim)
 
 
 def rms_norm(values, gain):
@@ -94,7 +116,7 @@
     key_low = key_turned.astype(jnp.bfloat16).reshape(tok_rows, groups * HD)
     key_all, value_all = (
         lax.all_gather(key_low, "wide", axis=0, tiled=True),
-        lax.all_gather(value_low, "wide", axis=0, tiled=True),
+        collect(value_low, "wide", 0),
     )
     key_all = key_all.reshape(total, groups, HD)
     value_all = value_all.reshape(total, groups, HD)

time: 1970 us -> 1880 us (0.954)
  waiting for transfers between devices: 1330 us -> 1200 us
  starting transfers between devices: 3.13 us -> 29.5 us
    all_gather x4 -> x0, waiting for transfers between devices: 65.8 us -> none  [one_batch(): lax.all_gather(value_low, 'wide', axis=0, tiled=True)]
    all_gather x4, waiting for transfers between devices: 74 us -> 17.8 us  [one_batch(): lax.all_gather(key_low, 'wide', axis=0, tiled=True)]
    ppermute x0 -> x28, waiting for transfers between devices: none -> 26.9 us  [the longest x16 21 us: collect(): lower.append(lax.ppermute(lower[-1] if lower else x, axis, pairs))]
    ppermute x0 -> x28, starting transfers between devices: none -> 26.6 us  [the longest x12 25.8 us: collect(): upper.append(lax.ppermute(upper[-1] if upper else x, axis, back))]
    unnamed x530 -> x586, local copies, waits for them, and re-layouts: 37 us -> 51.2 us
  transfers between devices with their start and end apart: 34 -> 58, of which waited for: 28 -> 33; matrix products, arithmetic and copies ran while one was open for 20% -> 21% of each run, Pallas kernels for 0% -> 0%
where the time goes in v1:
time: 1880 us; the launch traced here: 1870 us
  waiting for transfers between devices  1200 us (64%)
  matrix products  377 us (20%)
  other arithmetic  132 us (7%)
  local copies, waits for them, and re-layouts  72.7 us (4%)
  blocking collectives  39.5 us (2%)
  starting transfers between devices  29.5 us (2%)
    psum x1, waiting for transfers between devices, one_batch(): lax.psum(ffn_part.astype(jnp.bfloat16), 'narrow').astype(jnp.float32)  292 us
    psum x2, waiting for transfers between devices, one_batch(): lax.psum(attn_part.astype(jnp.bfloat16), 'narrow').astype(jnp.float32)  206 us
    reduce_scatter x4, waiting for transfers between devices, one_batch(): lax.psum_scatter(grad_valueall.reshape(total, groups * HD).astype(jnp.bfl...  129 us
    psum x1, waiting for transfers between devices, one_batch(): lax.psum(partial_two.astype(jnp.bfloat16), 'narrow').astype(jnp.float32)  119 us
    reduce_scatter x1, waiting for transfers between devices, local(): lax.psum_scatter(totals[4].astype(jnp.bfloat16), 'wide', scatter_dimensio...  64 us
    reduce_scatter x1, waiting for transfers between devices, local(): lax.psum_scatter(totals[5].astype(jnp.bfloat16), 'wide', scatter_dimensio...  62.7 us
    reduce_scatter x1, waiting for transfers between devices, local(): lax.psum_scatter(totals[6].astype(jnp.bfloat16), 'wide', scatter_dimensio...  62.6 us
    unnamed x586, local copies, waits for them, and re-layouts  51.2 us
  transfers between devices with their start and end apart: 58, of which 33 were waited for; matrix products, arithmetic and copies ran while one was open for 21% of the time, Pallas kernels for 0%

profile of v1, /device:TPU:0, one launch (start us, length us, event | category | flops | bytes accessed | tf_op | source)
XLA Modules:
  0.0 1867.6 jit_solution(13487367570994140306)
XLA Ops:
  15.6 20.4 %all-gather.14.cloned.1.call-done = bf16[2048,256]{1,0:T(8,128)(2,1)} async-done(((bf16[256,256]{1,0:T(8,128)(2,1)}), bf16[2048,256]{1,0:T(8,128)(2,1)}) %all-gather.14.cloned.1.call-update) | async-done | bytes 1048592 | tf_op jit(solution)/shard_map/all_gather | solution.py:270
  41.9 19.5 %all-gather.12.cloned.1.call-done = bf16[2048,256]{1,0:T(8,128)(2,1)} async-done(((bf16[256,256]{1,0:T(8,128)(2,1)}), bf16[2048,256]{1,0:T(8,128)(2,1)}) %all-gather.12.cloned.1.call-update) | async-done | bytes 1048592 | tf_op jit(solution)/shard_map/all_gather | solution.py:271
  103.4 17.7 all-gather.30.cloned.1.call-done
  128.9 22.1 %all-gather.20.cloned.1.call-done = bf16[512,2048]{1,0:T(8,128)(2,1)} async-done(((bf16[512,256]{1,0:T(8,128)(2,1)}), bf16[512,2048]{1,0:T(8,128)(2,1)}) %all-gather.20.cloned.1.call-update) | async-done | bytes 2097168 | tf_op jit(solution)/shard_map/all_gather | solution.py:272
  155.1 51.3 %all-reduce.25.cloned.1.call-done = bf16[256,2048]{1,0:T(8,128)(2,1)} async-done(((bf16[256,2048]{1,0:T(8,128)(2,1)}), bf16[256,2048]{1,0:T(8,128)(2,1)}) %all-reduce.25.cloned.1.call-update) | async-done | bytes 1048592 | tf_op jit(solution)/shard_map/psum | solution.py:132
  314.6 25.1 %all-gather.22.cloned.1.call-done = bf16[2048,1536]{1,0:T(8,128)(2,1)} async-done(((bf16[256,1536]{1,0:T(8,128)(2,1)}), bf16[2048,1536]{1,0:T(8,128)(2,1)}) %all-gather.22.cloned.1.call-update) | async-done | bytes 6291472 | tf_op jit(solution)/shard_map/all_gather | solution.py:273
  345.4 42.8 %all-gather.26.cloned.1.call-done = bf16[1536,2048]{1,0:T(8,128)(2,1)} async-done(((bf16[1536,256]{1,0:T(8,128)(2,1)}), bf16[1536,2048]{1,0:T(8,128)(2,1)}) %all-gather.26.cloned.1.call-update) | async-done | bytes 6291472 | tf_op jit(solution)/shard_map/all_gather | solution.py:275
  394.2 41.1 %all-gather.24.cloned.1.call-done = bf16[2048,1536]{1,0:T(8,128)(2,1)} async-done(((bf16[256,1536]{1,0:T(8,128)(2,1)}), bf16[2048,1536]{1,0:T(8,128)(2,1)}) %all-gather.24.cloned.1.call-update) | async-done | bytes 6291472 | tf_op jit(solution)/shard_map/all_gather | solution.py:274
  451.0 155.1 %all-reduce.31.cloned.1.call-done = (bf16[256,2048]{1,0:T(8,128)(2,1)}, bf16[256,2048]{1,0:T(8,128)(2,1)}, bf16[256,2048]{1,0:T(8,128)(2,1)}, bf16[256,2048]{1,0:T(8,128)(2,1)}) async-done(((bf16[256,2048]{1,0:T(8,128)(2,1)}, bf16[256,2048]{1,0:T(8,128)(2,1)}, bf16[256,2048]{1,0:T(8,128)(2,1)}, bf16[256,2048]{1,0:T(8,128)(2,1)}), (bf16[256,2048]{1,0:T(8,128)(2,1)}, bf16[256,2048]{1,0:T(8,128)(2,1)}, ...) | async-done | bytes 4194320 | tf_op jit(solution)/shard_map/psum | solution.py:132
  678.9 119.4 %all-reduce.29.cloned.1.call-done = (bf16[256,2048]{1,0:T(8,128)(2,1)}, bf16[256,2048]{1,0:T(8,128)(2,1)}, bf16[256,2048]{1,0:T(8,128)(2,1)}) async-done(((bf16[256,2048]{1,0:T(8,128)(2,1)}, bf16[256,2048]{1,0:T(8,128)(2,1)}, bf16[256,2048]{1,0:T(8,128)(2,1)}), (bf16[256,2048]{1,0:T(8,128)(2,1)}, bf16[256,2048]{1,0:T(8,128)(2,1)}, bf16[256,2048]{1,0:T(8,128)(2,1)})) %all-reduce.29.cloned.1.call-update) | async-done | bytes 3145744 | tf_op jit(solution)/shard_map/psum | solution.py:159
  966.4 15.1 reduce-scatter.20.cloned.1.call-done
  999.2 22.1 %reduce-scatter.18.cloned.1.call-done = bf16[256,256]{0,1:T(8,128)(2,1)} async-done(((bf16[2048,256]{0,1:T(8,128)(2,1)}), bf16[256,256]{0,1:T(8,128)(2,1)}) %reduce-scatter.18.cloned.1.call-update) | async-done | bytes 131088 | tf_op jit(solution)/shard_map/reduce_scatter | solution.py:190
  1024.4 35.9 %reduce-scatter.22.cloned.1.call-done = bf16[256,256]{0,1:T(8,128)(2,1)} async-done(((bf16[2048,256]{0,1:T(8,128)(2,1)}), bf16[256,256]{0,1:T(8,128)(2,1)}) %reduce-scatter.22.cloned.1.call-update) | async-done | bytes 131088 | tf_op jit(solution)/shard_map/reduce_scatter | solution.py:190
  1064.2 35.3 %reduce-scatter.26.cloned.1.call-done = bf16[256,256]{0,1:T(8,128)(2,1)} async-done(((bf16[2048,256]{0,1:T(8,128)(2,1)}), bf16[256,256]{0,1:T(8,128)(2,1)}) %reduce-scatter.26.cloned.1.call-update) | async-done | bytes 131088 | tf_op jit(solution)/shard_map/reduce_scatter | solution.py:190
  1103.3 35.8 %reduce-scatter.30.cloned.1.call-done = bf16[256,256]{0,1:T(8,128)(2,1)} async-done(((bf16[2048,256]{0,1:T(8,128)(2,1)}), bf16[256,256]{0,1:T(8,128)(2,1)}) %reduce-scatter.30.cloned.1.call-update) | async-done | bytes 131088 | tf_op jit(solution)/shard_map/reduce_scatter | solution.py:190
  1142.8 18.2 add_convert_fusion.2
  1182.1 17.4 add_convert_fusion.1
  1221.1 17.3 add_convert_fusion
  1280.1 27.2 %reduce-scatter.36.cloned.1.call-done = bf16[256,256]{1,0:T(8,128)(2,1)} async-done(((bf16[2048,256]{1,0:T(8,128)(2,1)}), bf16[256,256]{1,0:T(8,128)(2,1)}) %reduce-scatter.36.cloned.1.call-update) | async-done | bytes 131088 | tf_op jit(solution)/shard_map/reduce_scatter | solution.py:291
  1308.9 64.0 %reduce-scatter.40.cloned.1.call-done = bf16[256,1536]{1,0:T(8,128)(2,1)} async-done(((bf16[2048,1536]{1,0:T(8,128)(2,1)}), bf16[256,1536]{1,0:T(8,128)(2,1)}) %reduce-scatter.40.cloned.1.call-update) | async-done | bytes 786448 | tf_op jit(solution)/shard_map/reduce_scatter | solution.py:297
  1375.4 62.7 %reduce-scatter.42.cloned.1.call-done = bf16[256,1536]{1,0:T(8,128)(2,1)} async-done(((bf16[2048,1536]{1,0:T(8,128)(2,1)}), bf16[256,1536]{1,0:T(8,128)(2,1)}) %reduce-scatter.42.cloned.1.call-update) | async-done | bytes 786448 | tf_op jit(solution)/shard_map/reduce_scatter | solution.py:300
  1440.5 62.6 %reduce-scatter.44.cloned.1.call-done = bf16[1536,256]{1,0:T(8,128)(2,1)} async-done(((bf16[1536,2048]{1,0:T(8,128)(2,1)}), bf16[1536,256]{1,0:T(8,128)(2,1)}) %reduce-scatter.44.cloned.1.call-update) | async-done | bytes 786448 | tf_op jit(solution)/shard_map/reduce_scatter | solution.py:303
  1505.5 291.9 %all-reduce.27.cloned.1.call-done = (bf16[256,2048]{1,0:T(8,128)(2,1)}, bf16[256,2048]{1,0:T(8,128)(2,1)}, bf16[256,2048]{1,0:T(8,128)(2,1)}, bf16[256,2048]{1,0...) async-done(((bf16[256,2048]{1,0:T(8,128)(2,1)}, bf16[256,2048]{1,0:T(8,128)(2,1)}, ...) | async-done | bytes 8388624 | tf_op jit(solution)/shard_map/psum | solution.py:144
  1820.8 39.5 %all-reduce.16 = (f32[2048]{0:T(1024)}, f32[2048]{0:T(1024)}, f32[128]{0:T(128)}, f32[128]{0:T(128)}) all-reduce(f32[2048]{0:T(1024)S(1)} %add_add_fusion.17, f32[2048]{0:T(1024)S(1)} %add_add_fusion.16, f32[128]{0:T(128)S(1)} %add_add_fusion.19, f32[128]{0:T(128)S(1)} %add_add_fusion.18), channel_id=1, replica_groups=mesh['wide'=8,'narrow'=4] {'wide','narrow'}, use_global_device_ids=true, to_apply=%region_91.92 | all-reduce | flops 4352 | bytes 34816 | tf_op jit(solution)/shard_map/psum | solution.py:307
  (984 shorter events, 589.8 us)
Async XLA Ops:
  9.4 111.7 %all-gather.30.cloned.1.call-start = ((), (), s32[]{:S(2)}) async-start(), calls=%async_computation.24 | async-start | bytes 1179648 | tf_op jit(solution)/shard_map/all_gather | solution.py:118
  41.2 109.7 %all-gather.20.cloned.1.call-start = ((), (), s32[]{:S(2)}) async-start(), calls=%async_computation.19 | async-start | bytes 2359296 | tf_op jit(solution)/shard_map/all_gather | solution.py:272
  41.8 164.6 %all-reduce.25.cloned.1.call-start = ((), (), s32[]{:S(2)}) async-start(), calls=%async_computation.25 | async-start | bytes 2097152 | tf_op jit(solution)/shard_map/psum | solution.py:132
  154.3 129.6 %all-gather.32.cloned.1.call-start = ((), (), s32[]{:S(2)}) async-start(), calls=%async_computation.26 | async-start | bytes 1179648 | tf_op jit(solution)/shard_map/all_gather | solution.py:118
  217.1 122.6 %all-gather.22.cloned.1.call-start = ((), (), s32[]{:S(2)}) async-start(), calls=%async_computation.20 | async-start | bytes 7077888 | tf_op jit(solution)/shard_map/all_gather | solution.py:273
  217.7 170.5 %all-gather.26.cloned.1.call-start = ((), (), s32[]{:S(2)}) async-start(), calls=%async_computation.22 | async-start | bytes 7077888 | tf_op jit(solution)/shard_map/all_gather | solution.py:275
  218.4 216.9 %all-gather.24.cloned.1.call-start = ((), (), s32[]{:S(2)}) async-start(), calls=%async_computation.21 | async-start | bytes 7077888 | tf_op jit(solution)/shard_map/all_gather | solution.py:274
  219.0 387.1 %all-reduce.31.cloned.1.call-start = ((), (), s32[]{:S(2)}) async-start(), calls=%async_computation.44 | async-start | bytes 8388608 | tf_op jit(solution)/shard_map/psum | solution.py:132
  450.9 347.4 %all-reduce.29.cloned.1.call-start = ((), (), s32[]{:S(2)}) async-start(), calls=%async_computation.43 | async-start | bytes 6291456 | tf_op jit(solution)/shard_map/psum | solution.py:159
  678.1 277.9 %reduce-scatter.24.cloned.1.call-start = ((), (), s32[]{:S(2)}) async-start(), calls=%async_computation.31 | async-start | bytes 1179648 | tf_op jit(solution)/shard_map/reduce_scatter | solution.py:184
  828.6 129.1 %reduce-scatter.16.cloned.1.call-start = ((), (), s32[]{:S(2)}) async-start(), calls=%async_computation.27 | async-start | bytes 1179648 | tf_op jit(solution)/shard_map/reduce_scatter | solution.py:184
  866.8 114.7 %reduce-scatter.20.cloned.1.call-start = ((), (), s32[]{:S(2)}) async-start(), calls=%async_computation.29 | async-start | bytes 1179648 | tf_op jit(solution)/shard_map/reduce_scatter | solution.py:184
  876.9 144.3 %reduce-scatter.18.cloned.1.call-start = ((), (), s32[]{:S(2)}) async-start(), calls=%async_computation.28 | async-start | bytes 1179648 | tf_op jit(solution)/shard_map/reduce_scatter | solution.py:190
  888.2 172.0 %reduce-scatter.22.cloned.1.call-start = ((), (), s32[]{:S(2)}) async-start(), calls=%async_computation.30 | async-start | bytes 1179648 | tf_op jit(solution)/shard_map/reduce_scatter | solution.py:190
  899.0 200.4 %reduce-scatter.26.cloned.1.call-start = ((), (), s32[]{:S(2)}) async-start(), calls=%async_computation.32 | async-start | bytes 1179648 | tf_op jit(solution)/shard_map/reduce_scatter | solution.py:190
  911.0 228.2 %reduce-scatter.30.cloned.1.call-start = ((), (), s32[]{:S(2)}) async-start(), calls=%async_computation.34 | async-start | bytes 1179648 | tf_op jit(solution)/shard_map/reduce_scatter | solution.py:190
  925.0 349.7 %reduce-scatter.32.cloned.1.call-start = ((), (), s32[]{:S(2)}) async-start(), calls=%async_computation.35 | async-start | bytes 2359296 | tf_op jit(solution)/shard_map/reduce_scatter | solution.py:285
  933.5 342.9 %reduce-scatter.38.cloned.1.call-start = ((), (), s32[]{:S(2)}) async-start(), calls=%async_computation.38 | async-start | bytes 2359296 | tf_op jit(solution)/shard_map/reduce_scatter | solution.py:294
  956.0 322.5 %reduce-scatter.34.cloned.1.call-start = ((), (), s32[]{:S(2)}) async-start(), calls=%async_computation.36 | async-start | bytes 1179648 | tf_op jit(solution)/shard_map/reduce_scatter | solution.py:288
  991.2 316.1 %reduce-scatter.36.cloned.1.call-start = ((), (), s32[]{:S(2)}) async-start(), calls=%async_computation.37 | async-start | bytes 1179648 | tf_op jit(solution)/shard_map/reduce_scatter | solution.py:291
  1142.8 230.1 %reduce-scatter.40.cloned.1.call-start = ((), (), s32[]{:S(2)}) async-start(), calls=%async_computation.39 | async-start | bytes 7077888 | tf_op jit(solution)/shard_map/reduce_scatter | solution.py:297
  1161.0 277.0 %reduce-scatter.42.cloned.1.call-start = ((), (), s32[]{:S(2)}) async-start(), calls=%async_computation.40 | async-start | bytes 7077888 | tf_op jit(solution)/shard_map/reduce_scatter | solution.py:300
  1199.5 303.6 %reduce-scatter.44.cloned.1.call-start = ((), (), s32[]{:S(2)}) async-start(), calls=%async_computation.41 | async-start | bytes 7077888 | tf_op jit(solution)/shard_map/reduce_scatter | solution.py:303
  1238.5 558.9 %all-reduce.27.cloned.1.call-start = ((), (), s32[]{:S(2)}) async-start(), calls=%async_computation.42 | async-start | bytes 16777216 | tf_op jit(solution)/shard_map/psum | solution.py:144
  (313 other events, 3665.1 us)
Sparse Core Ops, SparseCore 0:
  63.2 32.0 all-gather.17
  122.8 28.0 all-gather.19
  154.4 51.8 all-reduce.24
  294.2 45.3 all-gather.21
  341.5 46.5 all-gather.25
  389.9 45.3 all-gather.23
  451.1 155.0 all-reduce.30
  678.2 120.0 all-reduce.28
  828.7 35.0 reduce-scatter.23
  867.4 35.9 reduce-scatter.15
  906.4 35.9 reduce-scatter.27
  945.5 35.9 reduce-scatter.19
  985.2 35.9 reduce-scatter.17
  1024.2 35.9 reduce-scatter.21
  1063.4 35.9 reduce-scatter.25
  1103.2 35.9 reduce-scatter.29
  1142.5 41.1 reduce-scatter.31
  1186.8 41.0 reduce-scatter.37
  1231.6 35.9 reduce-scatter.33
  1271.3 35.9 reduce-scatter.35
  1311.1 61.7 reduce-scatter.39
  1376.3 61.7 reduce-scatter.41
  1441.5 61.5 reduce-scatter.43
  1506.4 290.9 all-reduce.26
  (6 shorter events, 146.7 us)
